TPU v7x, 32 devices: a whole 2x2x4 slice. The times are simulated.
32 devices in a mesh: det: 8 (over y, x, core), bm: 4 (over z).
Axes of the slice: x: 2, y: 2, z: 4, core: 2. Of those that a mesh axis runs over, the one named last changes fastest.
Arguments:
- sky_alm: bfloat16 [2, 3, 16, 128], P(None, None, 'det'), may hold values from -6 to 6
- beam_blm: bfloat16 [2, 3, 16, 128], P(None, None, 'bm'), may hold values from -2.5 to 2.5
- wigner: bfloat16 [32, 16, 16, 128], P('det', None, 'bm'), may hold values from -0.03125 to 0.03125
- theta_index: int32 [128, 256], P('det'), may hold values from 0 to 3
- phi_index: int32 [128, 256], P('det'), may hold values from 0 to 16383
- psi_index: int32 [128, 256], P('det'), may hold values from 0 to 31
Outputs:
- tod: float32 [128, 256], P('det', 'bm')
All inputs are finite; a program needn't handle non-finite values.
Results may differ from a plain program's by a relative error of at most 0.0029.
Values may be sent and summed in bfloat16 or wider, within the bound.
A program may use at most 64 MiB of HBM per device.

v0:
```python
import math

import jax
import jax.numpy as jnp
from jax import lax
from jax.sharding import PartitionSpec as P

NPHI = 16384
NPSI = 32


TWO_PI = 2.0 * math.pi


def spectra_of(sky, beam):
    sky_full = sky.astype(jnp.float32)[:, :, :, None, :]
    beam_full = beam.astype(jnp.float32)[:, :, None, :, :]
    real_part = jnp.sum(sky_full[0] * beam_full[0] - sky_full[1] * beam_full[1], axis=0)
    imag_part = jnp.sum(sky_full[0] * beam_full[1] + sky_full[1] * beam_full[0], axis=0)
    return jnp.stack([real_part, imag_part]).astype(jnp.bfloat16)


def contract(table, spectra):
    return jnp.einsum("rmpl,kmpl->krpm", table, spectra, preferred_element_type=jnp.float32)


def product_first(left, right):
    dims = (((0,), (0,)), ((), ()))
    return lax.dot_general(
        left, right, dims, precision=lax.Precision.HIGHEST, preferred_element_type=jnp.float32
    )


def sample_tod(cube, theta, phi, psi):
    cycles = cube.shape[1]
    planes = cube.shape[2]
    modes = cube.shape[3]
    plane_ids = jnp.arange(planes, dtype=jnp.int32)
    psi_angle = TWO_PI * (plane_ids[:, None] * psi[None, :] % NPSI).astype(jnp.float32) / NPSI
    select = (theta[None, :] == jnp.arange(cycles, dtype=jnp.int32)[:, None]).astype(jnp.float32)
    cos_feat = (select[:, None, :] * jnp.cos(psi_angle)[None]).reshape(cycles * planes, -1)
    sin_feat = (select[:, None, :] * jnp.sin(psi_angle)[None]).reshape(cycles * planes, -1)
    flat = cube.reshape(2, cycles * planes, modes)
    k_real = product_first(flat[0], cos_feat) - product_first(flat[1], sin_feat)
    k_imag = product_first(flat[1], cos_feat) + product_first(flat[0], sin_feat)
    mode_ids = jnp.arange(modes, dtype=jnp.int32)
    phi_angle = TWO_PI * (mode_ids[:, None] * phi[None, :] % NPHI).astype(jnp.float32) / NPHI
    return jnp.sum(k_real * jnp.cos(phi_angle) - k_imag * jnp.sin(phi_angle), axis=0)


def on_device(sky_alm, beam_blm, wigner, theta_index, phi_index, psi_index):
    cube = contract(
        wigner, spectra_of(lax.all_gather(sky_alm, "det", axis=2, tiled=True), beam_blm)
    )
    all_planes = lax.all_gather(cube, "bm", axis=2, tiled=True)
    width = theta_index.shape[1] // lax.axis_size("bm")
    offset = lax.axis_index("bm") * width

    def columns(values):
        return lax.dynamic_slice_in_dim(values, offset, width, 1).reshape(-1)

    result = sample_tod(all_planes, columns(theta_index), columns(phi_index), columns(psi_index))
    return result.reshape(theta_index.shape[0], width)


def solution(mesh):
    placed = (
        P(None, None, "det", None),
        P(None, None, "bm", None),
        P("det", None, "bm", None),
        P("det", None),
        P("det", None),
        P("det", None),
    )
    return jax.shard_map(
        on_device, mesh=mesh, in_specs=placed, out_specs=P("det", "bm"), check_vma=False
    )
```

profile of v0, /device:TPU:0, one launch (start us, length us, event | category | flops | bytes accessed | tf_op | source)
XLA Modules:
  0.0 30.0 jit_solution(16744482656329492623)
XLA Ops:
  0.0 0.0 copy-start
  0.0 0.8 %constant_dynamic-slice_fusion = (s32[16,64]{1,0:T(8,128)S(1)}, s32[16,64]{1,0:T(8,128)S(1)}) fusion(s32[16,256]{1,0:T(8,128)} %param.10, s32[]{:T(128)S(6)} %select_n.23, s32[16,256]{1,0:T(8,128)} %param.11), kind=kLoop, calls=%fused_computation.43 | loop fusion | bytes 16388 | tf_op jit(solution)/shard_map/dynamic_slice | solution.py:60
  0.8 0.1 mul.167
  0.9 0.0 copy-start.2
  0.9 0.3 fusion.18
  1.2 0.4 %copy-done.2 = s32[16,256]{1,0:T(8,128)S(1)} copy-done((s32[16,256]{1,0:T(8,128)S(1)}, s32[16,256]{1,0:T(8,128)}, u32[]{:S(2)}) %copy-start.2) | copy-done | bytes 16408
  1.6 0.1 constant_dynamic-slice_fusion.2
  1.7 0.1 eq.22
  1.8 0.0 copy-start.3
  1.8 0.7 %copy-done.3 = bf16[2,3,2,128]{3,2,1,0:T(2,128)(2,1)S(1)} copy-done((bf16[2,3,2,128]{3,2,1,0:T(2,128)(2,1)S(1)}, bf16[2,3,2,128]{3,2,1,0:T(2,128)(2,1)}, u32[]{:S(2)}) %copy-start.3) | copy-done | bytes 3096
  2.5 10.6 %all_gather.6 = bf16[2,3,16,128]{3,0,1,2:T(2,128)(2,1)S(1)} all-gather(bf16[2,3,2,128]{3,0,1,2:T(2,128)(2,1)S(1)} %copy.30), channel_id=1, replica_groups=mesh['det'=8,'bm'=4] {'det'}, dimensions={2}, use_global_device_ids=true | all-gather | bytes 27648 | tf_op jit(solution)/shard_map/all_gather | solution.py:53
  13.1 0.0 copy-start.1
  13.1 0.7 %copy-done.1 = bf16[2,3,4,128]{3,2,1,0:T(4,128)(2,1)S(1)} copy-done((bf16[2,3,4,128]{3,2,1,0:T(4,128)(2,1)S(1)}, bf16[2,3,4,128]{3,2,1,0:T(4,128)(2,1)}, u32[]{:S(2)}) %copy-start.1) | copy-done | bytes 6168
  13.9 0.0 copy-done
  13.9 0.2 convolution_bitcast_fusion
  14.1 0.1 copy.35
  14.3 13.3 %all_gather.7 = f32[2,4,16,16]{3,1,0,2:T(4,128)S(1)} all-gather(f32[2,4,4,16]{3,1,0,2:T(4,128)S(1)} %copy.35), channel_id=1, replica_groups=mesh['det'=8,'bm'=4] {'bm'}, dimensions={2}, use_global_device_ids=true | all-gather | bytes 10240 | tf_op jit(solution)/shard_map/all_gather | solution.py:55
  27.6 0.1 copy.37
  27.7 0.1 squeeze.5
  27.8 0.3 fusion.24
  28.0 0.1 copy.36
  28.1 0.1 squeeze.4
  28.2 0.1 mul.177
  28.3 0.4 %fusion.2 = f32[16,1024]{1,0:T(8,128)S(1)} fusion(f32[16,1024]{1,0:T(8,128)S(1)} %fusion.24, f32[64,16]{0,1:T(8,128)S(1)} %squeeze.4, f32[64,1024]{1,0:T(8,128)S(1)} %bitcast.30, s32[1024]{0:T(1024)S(1)} %mul.177), kind=kOutput, calls=%fused_computation.5 | convolution fusion | flops 12845056 | bytes 401408 | tf_op jit(solution)/shard_map/dot_general | solution.py:29
  28.7 0.3 fusion.23
  28.9 0.4 %fusion.3 = f32[1024]{0:T(1024)S(1)} fusion(f32[16,1024]{1,0:T(8,128)S(1)} %fusion.2, f32[16,1024]{1,0:T(8,128)S(1)} %fusion.23, f32[64,16]{0,1:T(8,128)S(1)} %squeeze.5, f32[64,1024]{1,0:T(8,128)S(1)} %bitcast.31, s32[1024]{0:T(1024)S(1)} %mul.177), kind=kOutput, calls=%fused_computation.6 | convolution fusion | flops 12876800 | bytes 405504 | tf_op jit(solution)/shard_map/dot_general | solution.py:29
  29.3 0.7 %reshape.136 = f32[16,64]{1,0:T(8,128)} reshape(f32[1024]{0:T(1024)S(1)} %fusion.3) | data formatting | bytes 8192 | tf_op jit(solution)/shard_map/reshape | solution.py:63
  (11 shorter events, 0.2 us)
Async XLA Ops:
  0.0 13.9 %copy-start = (bf16[4,16,4,128]{3,2,1,0:T(4,128)(2,1)S(1)}, bf16[4,16,4,128]{3,2,1,0:T(4,128)(2,1)}, u32[]{:S(2)}) copy-start(bf16[4,16,4,128]{3,2,1,0:T(4,128)(2,1)} %param.8) | copy-start | bytes 196612
  0.9 0.7 %copy-start.2 = (s32[16,256]{1,0:T(8,128)S(1)}, s32[16,256]{1,0:T(8,128)}, u32[]{:S(2)}) copy-start(s32[16,256]{1,0:T(8,128)} %param.9) | copy-start | bytes 49156
  1.8 0.7 %copy-start.3 = (bf16[2,3,2,128]{3,2,1,0:T(2,128)(2,1)S(1)}, bf16[2,3,2,128]{3,2,1,0:T(2,128)(2,1)}, u32[]{:S(2)}) copy-start(bf16[2,3,2,128]{3,2,1,0:T(2,128)(2,1)} %param.6) | copy-start | bytes 9220
  13.1 0.7 %copy-start.1 = (bf16[2,3,4,128]{3,2,1,0:T(4,128)(2,1)S(1)}, bf16[2,3,4,128]{3,2,1,0:T(4,128)(2,1)}, u32[]{:S(2)}) copy-start(bf16[2,3,4,128]{3,2,1,0:T(4,128)(2,1)} %param.7) | copy-start | bytes 18436
where the time goes:
time: 30.4 us; the launch traced here: 30 us
  blocking collectives  23.9 us (79%)
  local copies, waits for them, and re-layouts  4.13 us (14%)
  matrix products  1.53 us (5%)
  other arithmetic  0.37 us (1%)
    all_gather x1, blocking collectives, on_device(): all_planes = lax.all_gather(cube, 'bm', axis=2, tiled=True)  13.3 us
    all_gather x1, blocking collectives, on_device(): lax.all_gather(sky_alm, 'det', axis=2, tiled=True)  10.6 us
    unnamed x9, local copies, waits for them, and re-layouts  1.81 us
    dot_general x4, matrix products, product_first(): lax.dot_general(left, right, dims, precision=lax.Precision.HIGHEST, prefe...  1.3 us
    dynamic_slice x2, local copies, waits for them, and re-layouts, columns(): return lax.dynamic_slice_in_dim(values, offset, width, 1).reshape(-1)  0.89 us
    reshape x1, local copies, waits for them, and re-layouts, on_device(): return result.reshape(theta_index.shape[0], width)  0.67 us

commit v1 on v0

v1 whole, which is shorter than its diff:
```python
import functools
import math

import jax
import jax.numpy as jnp
from jax import lax
from jax.experimental import pallas as pl
from jax.experimental.pallas import tpu as pltpu
from jax.sharding import PartitionSpec as P

NPHI = 16384
NPSI = 32

TWO_PI = 2.0 * math.pi
LANES = 128
ROWS = 8
F32 = jnp.float32
BF16 = jnp.bfloat16
MESH = pl.DeviceIdType.MESH


def cos_on_grid(step, grid):
    shift = (grid // 4).bit_length() - 1
    turn = (step + grid // 8) >> shift
    x = (step - (turn << shift)).astype(F32) * (TWO_PI / grid)
    x2 = x * x
    c = 1.0 + x2 * (-0.5 + x2 * (1 / 24 + x2 * (-1 / 720 + x2 * (1 / 40320))))
    s = x * (1.0 + x2 * (-1 / 6 + x2 * (1 / 120 + x2 * (-1 / 5040 + x2 * (1 / 362880)))))
    odd = (turn & 1) == 1
    value = jnp.where(odd, -s, c)
    return jnp.where((turn & 2) == 2, -value, value)


def partner(me, flip, n):
    out, bit = 0, 1
    while bit < n:
        digit = (me // bit) % 2
        out = out + bit * ((1 - digit) if flip & bit else digit)
        bit *= 2
    return out


def rows_of(values, groups, width):
    return jnp.concatenate([values[j * ROWS : (j + 1) * ROWS] for j in range(groups)], axis=1)


def kernel(
    n_det, n_bm,
    sky_hbm, beam_hbm, wig_hbm, theta_hbm, phi_hbm, psi_hbm, out_ref,
    sky_all, beam, wig, index, wide, feat, phase, cube_all,
    local_sem, sky_send, sky_recv, cube_send, cube_recv,
):
    det = lax.axis_index("det")
    bm = lax.axis_index("bm")
    local = [
        pltpu.make_async_copy(sky_hbm, sky_all.at[det], local_sem.at[0]),
        pltpu.make_async_copy(beam_hbm, beam, local_sem.at[1]),
        pltpu.make_async_copy(wig_hbm, wig, local_sem.at[2]),
        pltpu.make_async_copy(theta_hbm, index.at[0], local_sem.at[3]),
        pltpu.make_async_copy(phi_hbm, index.at[1], local_sem.at[4]),
        pltpu.make_async_copy(psi_hbm, index.at[2], local_sem.at[5]),
    ]
    for copy in local:
        copy.start()
    barrier = pltpu.get_barrier_semaphore()
    for flip in range(1, n_det):
        pl.semaphore_signal(
            barrier, inc=1, device_id=(partner(det, flip, n_det), bm), device_id_type=MESH
        )
    for step in range(1, n_bm):
        pl.semaphore_signal(
            barrier, inc=1, device_id=(det, (bm + step) % n_bm), device_id_type=MESH
        )
    local[0].wait()
    pl.semaphore_wait(barrier, n_det - 1 + n_bm - 1)
    sends = []
    for flip in range(n_det - 1, 0, -1):
        copy = pltpu.make_async_remote_copy(
            src_ref=sky_all.at[det],
            dst_ref=sky_all.at[det],
            send_sem=sky_send.at[flip],
            recv_sem=sky_recv.at[flip],
            device_id=(partner(det, flip, n_det), bm),
            device_id_type=MESH,
        )
        copy.start()
        sends.append(copy)
    for copy in local[1:]:
        copy.wait()

    cycles, flat, band = wig.shape
    planes = beam.shape[2]
    modes = flat // planes
    owned = sky_all.shape[3]
    pairs = cycles * planes
    depth = 2 * pairs
    per_tile = LANES // (2 * depth)
    tile_modes = per_tile * ROWS
    tiles = modes // tile_modes
    dets, samples = index.shape[1:]
    width = samples // n_bm
    groups = dets // ROWS

    for g in range(cycles):
        wide[g] = wig[g].astype(F32)

    def mine(values):
        own = values[:, :width]
        for i in range(1, n_bm):
            own = jnp.where(bm == i, values[:, i * width : (i + 1) * width], own)
        return rows_of(own, groups, width)

    theta, phi, psi = mine(index[0]), mine(index[1]), mine(index[2])
    span = groups * width
    k_rows = n_bm * depth
    row = lax.broadcasted_iota(jnp.int32, (k_rows, span), 0)
    plane = ((bm + row // depth) % n_bm) * planes + row % planes
    cycle = (row // planes) % cycles
    quarter = ((row // pairs) % 2) * (3 * NPSI // 4)
    m_rows = 2 * modes
    mrow = lax.broadcasted_iota(jnp.int32, (m_rows, span), 0)
    mode = (mrow // (2 * tile_modes)) * tile_modes + mrow % tile_modes
    mquarter = ((mrow // tile_modes) % 2) * (NPHI // 4)
    for j in range(ROWS):
        at = pl.ds(j * span, span)
        step = (plane * psi[j : j + 1] + quarter) & (NPSI - 1)
        value = jnp.where(cycle == theta[j : j + 1], cos_on_grid(step, NPSI), 0.0)
        high = value.astype(BF16)
        feat[:k_rows, at] = high
        feat[k_rows:, at] = (value - high.astype(F32)).astype(BF16)
        step = (mode * phi[j : j + 1] + mquarter) & (NPHI - 1)
        phase[:, at] = cos_on_grid(step, NPHI)

    for copy in sends:
        copy.wait_recv()

    lane = lax.broadcasted_iota(jnp.int32, (ROWS, LANES), 1)
    imag_row = (lane // (depth * per_tile)) % 2
    sin_column = (lane // pairs) % 2
    part = (imag_row + sin_column) % 2
    code = ((lane // depth) % per_tile * 2 + part) * pairs + lane % pairs
    sign = jnp.where((imag_row == 0) & (sin_column == 1), -1.0, 1.0)
    slots = tile_modes // owned
    for t in range(tiles):
        sky = [
            [
                sky_all[t * slots : (t + 1) * slots, r, c].astype(F32).reshape(tile_modes, band)
                for c in range(3)
            ]
            for r in range(2)
        ]
        packed = jnp.zeros((ROWS, LANES), F32)
        for h in range(per_tile):
            for p in range(planes):
                re = im = 0.0
                for c in range(3):
                    s0 = sky[0][c][h * ROWS : (h + 1) * ROWS]
                    s1 = sky[1][c][h * ROWS : (h + 1) * ROWS]
                    b0 = beam[0, c, p : p + 1].astype(F32)
                    b1 = beam[1, c, p : p + 1].astype(F32)
                    re = re + (s0 * b0 - s1 * b1)
                    im = im + (s0 * b1 + s1 * b0)
                re = re.astype(BF16).astype(F32)
                im = im.astype(BF16).astype(F32)
                first = (t * tile_modes + h * ROWS) * planes + p
                for g in range(cycles):
                    w = wide[g, pl.ds(first, ROWS, stride=planes)]
                    for k, spectra in enumerate((re, im)):
                        total = jnp.sum(w * spectra, axis=1, keepdims=True)
                        where = (h * 2 + k) * pairs + g * planes + p
                        packed = jnp.where(code == where, total, packed)
        cube_all[0, t] = packed * sign

    later = []
    for step in range(1, n_bm):
        copy = pltpu.make_async_remote_copy(
            src_ref=cube_all.at[0],
            dst_ref=cube_all.at[n_bm - step],
            send_sem=cube_send.at[n_bm - step],
            recv_sem=cube_recv.at[n_bm - step],
            device_id=(det, (bm + step) % n_bm),
            device_id_type=MESH,
        )
        copy.start()
        later.append(copy)
    for copy in later:
        copy.wait_recv()

    blocks = []
    for t in range(tiles):
        parts = [cube_all[s, t] for s in range(n_bm)]
        for q in range(2 * per_tile):
            blocks.append(
                jnp.concatenate([x[:, q * depth : (q + 1) * depth] for x in parts], axis=1)
            )
    left = jnp.concatenate(blocks, axis=0)
    high = left.astype(BF16)
    low = (left - high.astype(F32)).astype(BF16)
    both = jnp.concatenate(
        [jnp.concatenate([high, high], axis=1), jnp.concatenate([low, low], axis=1)], axis=0
    )
    for j in range(ROWS):
        at = pl.ds(j * span, span)
        y = jnp.dot(both, feat[:, at], preferred_element_type=F32)
        z = (y[:m_rows] + y[m_rows:]) * phase[:, at]
        total = jnp.sum(z, axis=0, keepdims=True)
        for i in range(groups):
            out_ref[pl.ds(i * ROWS + j, 1), :] = total[:, i * width : (i + 1) * width]

    for copy in sends + later:
        copy.wait_send()


def on_device(sky_alm, beam_blm, wigner, theta_index, phi_index, psi_index):
    n_det, n_bm = lax.axis_size("det"), lax.axis_size("bm")
    cycles, modes, planes, band = wigner.shape
    dets, samples = theta_index.shape
    width = samples // n_bm
    span = dets // ROWS * width
    depth = 2 * cycles * planes
    tiles = modes * 2 * depth // (ROWS * LANES)
    any_space = pl.BlockSpec(memory_space=pl.ANY)
    out = pl.pallas_call(
        functools.partial(kernel, n_det, n_bm),
        out_shape=jax.ShapeDtypeStruct((dets, width), F32),
        in_specs=[any_space] * 6,
        out_specs=pl.BlockSpec(memory_space=pltpu.VMEM),
        scratch_shapes=[
            pltpu.VMEM((n_det, *sky_alm.shape), BF16),
            pltpu.VMEM(beam_blm.shape, BF16),
            pltpu.VMEM((cycles, modes * planes, band), BF16),
            pltpu.VMEM((3, dets, samples), jnp.int32),
            pltpu.VMEM((cycles, modes * planes, band), F32),
            pltpu.VMEM((2 * n_bm * depth, ROWS * span), BF16),
            pltpu.VMEM((2 * modes, ROWS * span), F32),
            pltpu.VMEM((n_bm, tiles, ROWS, LANES), F32),
            pltpu.SemaphoreType.DMA((6,)),
            pltpu.SemaphoreType.DMA((n_det,)),
            pltpu.SemaphoreType.DMA((n_det,)),
            pltpu.SemaphoreType.DMA((n_bm,)),
            pltpu.SemaphoreType.DMA((n_bm,)),
        ],
        compiler_params=pltpu.CompilerParams(collective_id=0, has_side_effects=True),
    )(
        sky_alm,
        beam_blm,
        wigner.reshape(cycles, modes * planes, band),
        theta_index,
        phi_index,
        psi_index,
    )
    return out


def solution(mesh):
    placed = (
        P(None, None, "det", None),
        P(None, None, "bm", None),
        P("det", None, "bm", None),
        P("det", None),
        P("det", None),
        P("det", None),
    )
    return jax.shard_map(
        on_device, mesh=mesh, in_specs=placed, out_specs=P("det", "bm"), check_vma=False
    )
```

time: 30.4 us -> 14.4 us (0.47)
  blocking collectives: 23.9 us -> 0 us
  Pallas kernels: 0 us -> 12.9 us
  local copies, waits for them, and re-layouts: 4.13 us -> 1.3 us
  matrix products: 1.53 us -> 0 us
  other arithmetic: 0.37 us -> 0 us
    all_gather x2 -> x0, blocking collectives: 23.9 us -> none  [the longest x1 13.3 us: on_device(): all_planes = lax.all_gather(cube, 'bm', axis=2, tiled=True)]
    pallas_call x0 -> x1, Pallas kernels: none -> 12.9 us  [on_device(): pl.pallas_call(functools.partial(kernel, n_det, n_bm), out_shape=jax.Shap...]
    dot_general x5 -> x0, matrix products: 1.53 us -> none  [the longest x4 1.3 us: product_first(): lax.dot_general(left, right, dims, precision=lax.Precision.HIGHEST, prefe...]
    dynamic_slice x2 -> x0, local copies, waits for them, and re-layouts: 0.89 us -> none  [columns(): return lax.dynamic_slice_in_dim(values, offset, width, 1).reshape(-1)]
    reshape x1 -> x0, local copies, waits for them, and re-layouts: 0.67 us -> none  [on_device(): return result.reshape(theta_index.shape[0], width)]
    unnamed x9 -> x1, local copies, waits for them, and re-layouts: 1.81 us -> 1.3 us
where the time goes in v1:
time: 14.4 us; the launch traced here: 14.2 us
  Pallas kernels  12.9 us (90%)
  local copies, waits for them, and re-layouts  1.3 us (9%)
    pallas_call x1, Pallas kernels, on_device(): pl.pallas_call(functools.partial(kernel, n_det, n_bm), out_shape=jax.Shap...  12.9 us
    unnamed x1, local copies, waits for them, and re-layouts  1.3 us

profile of v1, /device:TPU:0, one launch (start us, length us, event | category | flops | bytes accessed | tf_op | source)
XLA Modules:
  0.0 14.2 jit_solution(17241643163488275814)
XLA Ops:
  0.0 12.9 %shard_map.64 = f32[16,64]{1,0:T(8,128)} custom-call(bf16[2,3,2,128]{3,2,1,0:T(2,128)(2,1)} %sky_hbm.1, bf16[2,3,4,128]{3,2,1,0:T(4,128)(2,1)} %beam_hbm.1, bf16[4,64,128]{2,1,0:T(8,128)(2,1)} %bitcast.1, s32[16,256]{1,0:T(8,128)} %theta_hbm.1, s32[16,256]{1,0:T(8,128)} %phi_hbm.1, s32[16,256]{1,0:T(8,128)} %psi_hbm.1), custom_call_target="tpu_custom_call" | custom-call | tf_op jit(solution)/shard_map/pallas_call | solution.py:223
  12.9 1.3 %copy.8 = f32[16,64]{1,0:T(8,128)} copy(f32[16,64]{1,0:T(8,128)} %shard_map.64) | data formatting | bytes 8192

commit v2 on v1

--- a/solution.py
+++ b/solution.py
@@ -48,7 +48,7 @@
     n_det, n_bm,
     sky_hbm, beam_hbm, wig_hbm, theta_hbm, phi_hbm, psi_hbm, out_ref,
     sky_all, beam, wig, index, wide, feat, phase, cube_all,
-    local_sem, sky_send, sky_recv, cube_send, cube_recv,
+    local_sem, sky_send, sky_recv, cube_send, cube_recv, ready,
 ):
     det = lax.axis_index("det")
     bm = lax.axis_index("bm")
@@ -67,12 +67,14 @@
         pl.semaphore_signal(
             barrier, inc=1, device_id=(partner(det, flip, n_det), bm), device_id_type=MESH
         )
-    for step in range(1, n_bm):
+    relayed = n_bm == 4
+    greeted = (1, 2) if relayed else range(1, n_bm)
+    for flip in greeted:
         pl.semaphore_signal(
-            barrier, inc=1, device_id=(det, (bm + step) % n_bm), device_id_type=MESH
+            barrier, inc=1, device_id=(det, partner(bm, flip, n_bm)), device_id_type=MESH
         )
     local[0].wait()
-    pl.semaphore_wait(barrier, n_det - 1 + n_bm - 1)
+    pl.semaphore_wait(barrier, n_det - 1 + len(greeted))
     sends = []
     for flip in range(n_det - 1, 0, -1):
         copy = pltpu.make_async_remote_copy(
@@ -85,6 +87,10 @@
         )
         copy.start()
         sends.append(copy)
+    if relayed:
+        pl.semaphore_signal(
+            ready, inc=1, device_id=(det, partner(bm, 1, n_bm)), device_id_type=MESH
+        )
     for copy in local[1:]:
         copy.wait()
 
@@ -114,7 +120,10 @@
     span = groups * width
     k_rows = n_bm * depth
     row = lax.broadcasted_iota(jnp.int32, (k_rows, span), 0)
-    plane = ((bm + row // depth) % n_bm) * planes + row % planes
+    source = 0
+    for flip in range(n_bm):
+        source = jnp.where(row // depth == flip, partner(bm, flip, n_bm), source)
+    plane = source * planes + row % planes
     cycle = (row // planes) % cycles
     quarter = ((row // pairs) % 2) * (3 * NPSI // 4)
     m_rows = 2 * modes
@@ -172,13 +181,15 @@
         cube_all[0, t] = packed * sign
 
     later = []
-    for step in range(1, n_bm):
+    if relayed:
+        pl.semaphore_wait(ready, 1)
+    for flip in range(n_bm - 1, 0, -1):
         copy = pltpu.make_async_remote_copy(
             src_ref=cube_all.at[0],
-            dst_ref=cube_all.at[n_bm - step],
-            send_sem=cube_send.at[n_bm - step],
-            recv_sem=cube_recv.at[n_bm - step],
-            device_id=(det, (bm + step) % n_bm),
+            dst_ref=cube_all.at[flip],
+            send_sem=cube_send.at[flip],
+            recv_sem=cube_recv.at[flip],
+            device_id=(det, partner(bm, flip, n_bm)),
             device_id_type=MESH,
         )
         copy.start()
@@ -199,13 +210,13 @@
     both = jnp.concatenate(
         [jnp.concatenate([high, high], axis=1), jnp.concatenate([low, low], axis=1)], axis=0
     )
+    y = jnp.dot(both, feat[...], preferred_element_type=F32)
+    z = (y[:m_rows] + y[m_rows:]) * phase[...]
+    total = jnp.sum(z, axis=0, keepdims=True)
     for j in range(ROWS):
-        at = pl.ds(j * span, span)
-        y = jnp.dot(both, feat[:, at], preferred_element_type=F32)
-        z = (y[:m_rows] + y[m_rows:]) * phase[:, at]
-        total = jnp.sum(z, axis=0, keepdims=True)
         for i in range(groups):
-            out_ref[pl.ds(i * ROWS + j, 1), :] = total[:, i * width : (i + 1) * width]
+            at = j * span + i * width
+            out_ref[pl.ds(i * ROWS + j, 1), :] = total[:, at : at + width]
 
     for copy in sends + later:
         copy.wait_send()
@@ -222,7 +233,7 @@
     any_space = pl.BlockSpec(memory_space=pl.ANY)
     out = pl.pallas_call(
         functools.partial(kernel, n_det, n_bm),
-        out_shape=jax.ShapeDtypeStruct((dets, width), F32),
+        out_shape=pltpu.VMEM((dets, width), F32),
         in_specs=[any_space] * 6,
         out_specs=pl.BlockSpec(memory_space=pltpu.VMEM),
         scratch_shapes=[
@@ -239,6 +250,7 @@
             pltpu.SemaphoreType.DMA((n_det,)),
             pltpu.SemaphoreType.DMA((n_bm,)),
             pltpu.SemaphoreType.DMA((n_bm,)),
+            pltpu.SemaphoreType.REGULAR,
         ],
         compiler_params=pltpu.CompilerParams(collective_id=0, has_side_effects=True),
     )(

time: 14.4 us -> 13.1 us (0.910)
  local copies, waits for them, and re-layouts: 1.3 us -> 0.6 us
  Pallas kernels: 12.9 us -> 12.3 us
    unnamed x1, local copies, waits for them, and re-layouts: 1.3 us -> 0.6 us
    pallas_call x1, Pallas kernels: 12.9 us -> 12.3 us  [on_device(): pl.pallas_call(functools.partial(kernel, n_det, n_bm), out_shape=pltpu.VM...]
where the time goes in v2:
time: 13.1 us; the launch traced here: 12.9 us
  Pallas kernels  12.3 us (94%)
  local copies, waits for them, and re-layouts  0.6 us (5%)
    pallas_call x1, Pallas kernels, on_device(): pl.pallas_call(functools.partial(kernel, n_det, n_bm), out_shape=pltpu.VM...  12.3 us
    unnamed x1, local copies, waits for them, and re-layouts  0.6 us

profile of v2, /device:TPU:0, one launch (start us, length us, event | category | flops | bytes accessed | tf_op | source)
XLA Modules:
  0.0 12.9 jit_solution(3180615980578529281)
XLA Ops:
  0.0 12.3 %shard_map.64 = f32[16,64]{1,0:T(8,128)S(1)} custom-call(bf16[2,3,2,128]{3,2,1,0:T(2,128)(2,1)} %sky_hbm.1, bf16[2,3,4,128]{3,2,1,0:T(4,128)(2,1)} %beam_hbm.1, bf16[4,64,128]{2,1,0:T(8,128)(2,1)} %bitcast.1, s32[16,256]{1,0:T(8,128)} %theta_hbm.1, s32[16,256]{1,0:T(8,128)} %phi_hbm.1, s32[16,256]{1,0:T(8,128)} %psi_hbm.1), custom_call_target="tpu_custom_call" | custom-call | tf_op jit(solution)/shard_map/pallas_call | solution.py:234
  12.3 0.6 %copy.8 = f32[16,64]{1,0:T(8,128)} copy(f32[16,64]{1,0:T(8,128)S(1)} %shard_map.64) | data formatting | bytes 8192

commit v3 on v2

--- a/solution.py
+++ b/solution.py
@@ -140,38 +140,46 @@
         step = (mode * phi[j : j + 1] + mquarter) & (NPHI - 1)
         phase[:, at] = cos_on_grid(step, NPHI)
 
-    for copy in sends:
-        copy.wait_recv()
-
     lane = lax.broadcasted_iota(jnp.int32, (ROWS, LANES), 1)
     imag_row = (lane // (depth * per_tile)) % 2
     sin_column = (lane // pairs) % 2
     part = (imag_row + sin_column) % 2
     code = ((lane // depth) % per_tile * 2 + part) * pairs + lane % pairs
     sign = jnp.where((imag_row == 0) & (sin_column == 1), -1.0, 1.0)
-    slots = tile_modes // owned
+    slots = ROWS // owned
+    halves = tiles == 1 and per_tile == 2 and slots * 2 == n_det and n_det & (n_det - 1) == 0
+    arriving = sends[::-1]
+    if not halves:
+        for copy in arriving:
+            copy.wait_recv()
     for t in range(tiles):
-        sky = [
-            [
-                sky_all[t * slots : (t + 1) * slots, r, c].astype(F32).reshape(tile_modes, band)
-                for c in range(3)
+        packed = jnp.zeros((ROWS, LANES), F32)
+        for turn in range(per_tile):
+            h = turn
+            if halves:
+                h = (det // slots + turn) % 2
+                for copy in arriving[slots - 1 :] if turn else arriving[: slots - 1]:
+                    copy.wait_recv()
+            block = t * per_tile + h
+            sky = [
+                [
+                    sky_all[pl.ds(block * slots, slots), r, c].astype(F32).reshape(ROWS, band)
+                    for c in range(3)
+                ]
+                for r in range(2)
             ]
-            for r in range(2)
-        ]
-        packed = jnp.zeros((ROWS, LANES), F32)
-        for h in range(per_tile):
             for p in range(planes):
                 re = im = 0.0
                 for c in range(3):
-                    s0 = sky[0][c][h * ROWS : (h + 1) * ROWS]
-                    s1 = sky[1][c][h * ROWS : (h + 1) * ROWS]
+                    s0 = sky[0][c]
+                    s1 = sky[1][c]
                     b0 = beam[0, c, p : p + 1].astype(F32)
                     b1 = beam[1, c, p : p + 1].astype(F32)
                     re = re + (s0 * b0 - s1 * b1)
                     im = im + (s0 * b1 + s1 * b0)
                 re = re.astype(BF16).astype(F32)
                 im = im.astype(BF16).astype(F32)
-                first = (t * tile_modes + h * ROWS) * planes + p
+                first = block * (ROWS * planes) + p
                 for g in range(cycles):
                     w = wide[g, pl.ds(first, ROWS, stride=planes)]
                     for k, spectra in enumerate((re, im)):
@@ -194,16 +202,19 @@
         )
         copy.start()
         later.append(copy)
-    for copy in later:
-        copy.wait_recv()
-
     blocks = []
-    for t in range(tiles):
-        parts = [cube_all[s, t] for s in range(n_bm)]
-        for q in range(2 * per_tile):
-            blocks.append(
-                jnp.concatenate([x[:, q * depth : (q + 1) * depth] for x in parts], axis=1)
-            )
+    for flip in range(n_bm):
+        if flip:
+            later[n_bm - 1 - flip].wait_recv()
+        for t in range(tiles):
+            x = cube_all[flip, t]
+            for q in range(2 * per_tile):
+                piece = x[:, q * depth : (q + 1) * depth]
+                at = t * 2 * per_tile + q
+                if flip:
+                    blocks[at] = jnp.concatenate([blocks[at], piece], axis=1)
+                else:
+                    blocks.append(piece)
     left = jnp.concatenate(blocks, axis=0)
     high = left.astype(BF16)
     low = (left - high.astype(F32)).astype(BF16)

time: 13.1 us -> 13.1 us (level)
  no operation moved by 1% of the time
where the time goes in v3:
time: 13.1 us; the launch traced here: 12.9 us
  Pallas kernels  12.3 us (94%)
  local copies, waits for them, and re-layouts  0.6 us (5%)
    pallas_call x1, Pallas kernels, on_device(): pl.pallas_call(functools.partial(kernel, n_det, n_bm), out_shape=pltpu.VM...  12.3 us
    unnamed x1, local copies, waits for them, and re-layouts  0.6 us

profile of v3, /device:TPU:0, one launch (start us, length us, event | category | flops | bytes accessed | tf_op | source)
XLA Modules:
  0.0 12.9 jit_solution(6968426581126926575)
XLA Ops:
  0.0 12.3 %shard_map.64 = f32[16,64]{1,0:T(8,128)S(1)} custom-call(bf16[2,3,2,128]{3,2,1,0:T(2,128)(2,1)} %sky_hbm.1, bf16[2,3,4,128]{3,2,1,0:T(4,128)(2,1)} %beam_hbm.1, bf16[4,64,128]{2,1,0:T(8,128)(2,1)} %bitcast.1, s32[16,256]{1,0:T(8,128)} %theta_hbm.1, s32[16,256]{1,0:T(8,128)} %phi_hbm.1, s32[16,256]{1,0:T(8,128)} %psi_hbm.1), custom_call_target="tpu_custom_call" | custom-call | tf_op jit(solution)/shard_map/pallas_call | solution.py:245
  12.3 0.6 %copy.8 = f32[16,64]{1,0:T(8,128)} copy(f32[16,64]{1,0:T(8,128)S(1)} %shard_map.64) | data formatting | bytes 8192
